TPU v7x, 32 devices: a whole 2x2x4 slice. The times are simulated.
32 devices in a mesh: facet: 8 (over z, y), freq: 4 (over x, core).
Axes of the slice: x: 2, y: 2, z: 4, core: 2. Of those that a mesh axis runs over, the one named last changes fastest.
Arguments:
- visibilities: bfloat16 [4, 2048, 2, 512], P('freq', 'facet'), may hold values from -6 to 6
- uvw: bfloat16 [4, 2048, 3, 512], P('freq', 'facet'), may hold values from -4 to 4
- facet_of: int32 [4, 2048, 1], P('freq', 'facet'), may hold values from 0 to 7; in each aligned block of 256 rows (0 to 255, 256 to 511, ..., all dimensions but the last counted through in order) at most 128 rows name the same one
- plane_of: int32 [4, 2048], P('freq', 'facet'), may hold values from 0 to 7
- cell_of: int32 [4, 2048], P('freq', 'facet'), may hold values from 0 to 1023
- kernels: bfloat16 [8, 2, 512, 256], replicated, may hold values from -0.25 to 0.25
- centers: float32 [8, 2], replicated, may hold values from -0.4 to 0.4
Outputs:
- images: float32 [8, 512, 512], P('facet', None, 'freq')
Inputs may be any that keep to these rules, and one draw needn't show every extreme that they name: `facet_of`: the facet index k is held by index k of the facet axis. In each aligned block of 256 tiles of one group, no facet is named by more than 128 tiles, and in some blocks one facet is named by exactly 128.
All inputs are finite; a program needn't handle non-finite values.
Results may differ from a plain program's by a relative error of at most 0.0095.
Values may be sent and summed in bfloat16 or wider, within the bound.
No kernel may reach another device: no remote copies, remote signals or barrier semaphores. Data moves between devices by JAX's collectives and lax.ppermute only.
A program may use at most 128 MiB of HBM per device.

v0:
```python
import jax
import jax.numpy as jnp
from jax import lax
from jax.sharding import PartitionSpec as P

GRID = 512
PSIDE = 16


def dft_tables(length):
    indices = jnp.arange(length, dtype=jnp.int32)
    products_mod = indices[:, None] * indices[None, :] % length
    angle_table = products_mod.astype(jnp.float32) * (2.0 * jnp.pi / length)
    norm_scale = 1.0 / jnp.sqrt(jnp.float32(length))
    table_real = (jnp.cos(angle_table) * norm_scale).astype(jnp.bfloat16)
    table_imag = (jnp.sin(angle_table) * norm_scale).astype(jnp.bfloat16)
    return (table_real, table_imag)


def rotate_tiles(vis_pair, coords, sky_pos):
    l_coord = sky_pos[:, 0:1]
    m_coord = sky_pos[:, 1:2]
    w_term = jnp.sqrt(1.0 - l_coord * l_coord - m_coord * m_coord) - 1.0
    coords = coords.astype(jnp.float32)
    phase_angle = (
        2.0 * jnp.pi * (l_coord * coords[:, 0] + m_coord * coords[:, 1] + w_term * coords[:, 2])
    )
    cosine = jnp.cos(phase_angle)
    sine_part = jnp.sin(phase_angle)
    real_part = vis_pair[:, 0].astype(jnp.float32)
    imag_part = vis_pair[:, 1].astype(jnp.float32)
    rot_real = (real_part * cosine + imag_part * sine_part).astype(jnp.bfloat16)
    rot_imag = (imag_part * cosine - real_part * sine_part).astype(jnp.bfloat16)
    return (rot_real, rot_imag)


def stack_kernels(kernels):
    kern_real = kernels[:, 0]
    kern_imag = kernels[:, 1]
    upper_rows = jnp.concatenate([kern_real, kern_imag], axis=2)
    lower_rows = jnp.concatenate([-kern_imag, kern_real], axis=2)
    stacked_rows = jnp.concatenate([upper_rows, lower_rows], axis=0)
    return stacked_rows.reshape(-1, stacked_rows.shape[2])


def grid_tiles(rot_real, rot_imag, planes, stacked, plane_count):
    plane_select = (planes[:, None] == jnp.arange(plane_count)[None, :]).astype(jnp.bfloat16)
    spread = jnp.concatenate(
        [
            rot_real[:, None, :] * plane_select[:, :, None],
            rot_imag[:, None, :] * plane_select[:, :, None],
        ],
        axis=1,
    )
    spread = spread.reshape(spread.shape[0], -1)
    return jnp.dot(spread, stacked, preferred_element_type=jnp.float32).astype(jnp.bfloat16)


def shards(visibilities, uvw, facet_of, plane_of, cell_of, kernels, centers):
    peer_count = lax.axis_size("facet")
    tile_count = visibilities.shape[1]
    capacity = 4 * tile_count // peer_count
    total_slots = peer_count * capacity
    vis_pair = visibilities[0]
    coords = uvw[0]
    target = facet_of[0, :, 0]
    planes = plane_of[0]
    tile_cells = cell_of[0]
    plane_count = kernels.shape[0]
    stacked = stack_kernels(kernels)
    dest_hits = (target[:, None] == jnp.arange(peer_count)[None, :]).astype(jnp.int32)
    before = jnp.cumsum(dest_hits, axis=0) - dest_hits
    within_rank = jnp.sum(before * dest_hits, axis=1)
    slot_index = target * capacity + within_rank
    chosen = (target[:, None] == jnp.arange(centers.shape[0])[None, :]).astype(jnp.float32)
    sky_rows = jnp.sum(chosen[:, :, None] * centers[None, :, :], axis=1)
    rot_real, rot_imag = rotate_tiles(vis_pair, coords, sky_rows)
    own_patches = grid_tiles(rot_real, rot_imag, planes, stacked, plane_count)
    patch_buffer = (
        jnp.zeros((total_slots, own_patches.shape[1]), jnp.bfloat16).at[slot_index].set(own_patches)
    )
    cell_buffer = jnp.zeros((total_slots,), jnp.int32).at[slot_index].set(tile_cells)
    patches, slot_cells = (
        lax.all_to_all(
            patch_buffer.reshape(peer_count, capacity, -1),
            "facet",
            split_axis=0,
            concat_axis=0,
            tiled=True,
        ),
        lax.all_to_all(
            cell_buffer.reshape(peer_count, capacity),
            "facet",
            split_axis=0,
            concat_axis=0,
            tiled=True,
        ),
    )
    patches = patches.reshape(-1, patches.shape[-1])
    slot_cells = slot_cells.reshape(-1)
    nblocks = GRID // PSIDE
    ncells = nblocks * nblocks
    placing = (slot_cells[None, :] == jnp.arange(ncells)[:, None]).astype(jnp.bfloat16)
    blocks = jnp.dot(placing, patches, preferred_element_type=jnp.float32).astype(jnp.bfloat16)
    uv_grid = (
        blocks.reshape(nblocks, nblocks, 2, PSIDE, PSIDE)
        .transpose(2, 0, 3, 1, 4)
        .reshape(2 * GRID, GRID)
    )
    table_real, table_imag = dft_tables(GRID)
    table_both = jnp.concatenate([table_real, table_imag], axis=1)
    product = jnp.dot(uv_grid, table_both, preferred_element_type=jnp.float32)
    half_real = product[:GRID, :GRID] - product[GRID:, GRID:]
    half_imag = product[:GRID, GRID:] + product[GRID:, :GRID]
    partial_value = jnp.stack([half_real, half_imag]).astype(jnp.bfloat16)
    summed = lax.psum_scatter(
        partial_value.astype(jnp.float32).astype(jnp.bfloat16),
        "freq",
        scatter_dimension=2,
        tiled=True,
    )
    right_side = jnp.concatenate([summed[0], -summed[1]], axis=0)
    facet_image = jnp.dot(table_both, right_side, preferred_element_type=jnp.float32)
    return facet_image[None]


def solution(mesh):
    in_specs = (
        P("freq", "facet", None, None),
        P("freq", "facet", None, None),
        P("freq", "facet", None),
        P("freq", "facet"),
        P("freq", "facet"),
        P(),
        P(),
    )
    out_specs = P("facet", None, "freq")
    return jax.shard_map(shards, mesh=mesh, in_specs=in_specs, out_specs=out_specs, check_vma=False)
```

profile of v0, /device:TPU:0, one launch (start us, length us, event | category | flops | bytes accessed | tf_op | source)
XLA Modules:
  0.0 132.8 jit_solution(11374898481415891809)
XLA Ops:
  6.5 0.7 fusion.52
  7.2 0.6 reduce-window.6
  8.0 0.8 fusion.50
  8.8 0.7 compare_select_fusion
  9.5 2.1 %scatter_custom_fusion = s32[1024]{0:T(1024)} fusion(s32[256]{0:T(256)S(1)} %bitcast.85, s32[256]{0:T(256)} %bitcast.87, s32[]{:T(128)} %constant.12.clone.1), kind=kCustom, calls=%fused_computation.80 | custom fusion | bytes 4608 | tf_op jit(solution)/shard_map/scatter | solution.py:82
  11.6 7.3 %all-to-all-start = ((s32[8,1,128]{2,1,0:T(1,128)}), s32[8,1,128]{2,1,0:T(1,128)S(1)}, u32[]{:S(2)}, u32[]{:S(2)}) async-start(s32[8,1,128]{2,1,0:T(1,128)} %bitcast.8), calls=%async_computation | async-start | bytes 8192 | tf_op jit(solution)/shard_map/all_to_all | solution.py:91
  18.9 0.7 fusion.51
  19.6 2.7 %slice_bitcast_fusion = (bf16[8,512,256]{2,1,0:T(8,128)(2,1)S(1)}, bf16[8,512,256]{2,1,0:T(8,128)(2,1)S(1)}) fusion(bf16[8,2,512,256]{3,2,1,0:T(8,128)(2,1)} %param.12), kind=kLoop, calls=%fused_computation.15 | loop fusion | bytes 8388608 | tf_op jit(solution)/shard_map/squeeze | solution.py:39
  22.4 0.7 copy-done
  23.2 0.5 copy-done.4
  24.4 0.4 copy-done.2
  24.9 2.1 %fusion.60 = (f32[256,1,512]{2,0,1:T(8,128)S(1)}, f32[256,1,512]{2,0,1:T(8,128)S(1)}) fusion(f32[256,3,512]{2,0,1:T(8,128)S(1)} %bitcast_convert_fusion, f32[256]{0:T(256)S(1)} %bitcast.80, f32[256]{0:T(256)S(1)} %bitcast.81, f32[256]{0:T(256)S(1)} %bitcast.79), kind=kLoop, calls=%fused_computation.88 | loop fusion | flops 786432 | bytes 2624512 | tf_op jit(solution)/shard_map/cos | solution.py:28
  27.1 1.9 %fusion.45 = (bf16[256,512]{1,0:T(8,128)(2,1)S(1)}, bf16[256,512]{1,0:T(8,128)(2,1)S(1)}) fusion(f32[256,1,512]{2,0,1:T(8,128)S(1)} %get-tuple-element.5, bf16[256,2,512]{2,0,1:T(8,128)(2,1)S(1)} %bitcast.73, f32[256,1,512]{2,0,1:T(8,128)S(1)} %get-tuple-element.6), kind=kLoop, calls=%fused_computation.63 | loop fusion | flops 1310720 | bytes 2097152 | tf_op jit(solution)/shard_map/mul | solution.py:50
  29.0 0.4 broadcast_multiply_fusion.1
  29.4 2.3 %fusion.19 = bf16[256,512]{1,0:T(8,128)(2,1)S(1)} fusion(bf16[8,512,256]{2,1,0:T(8,128)(2,1)S(1)} %get-tuple-element.10, bf16[8,512,256]{2,1,0:T(8,128)(2,1)S(1)} %fusion.59, bf16[8,512,256]{2,1,0:T(8,128)(2,1)S(1)} %get-tuple-element.9, bf16[256,8,512]{2,0,1:T(8,128)(2,1)S(1)} %get-tuple-element.16, bf16[256,8,512]{2,0,1:T(8,128)(2,1)S(1)} %get-tuple-element.15), kind=kOutput, calls=%fused_computation.23 | convolution fusion | flops 2183266304 | bytes 10747904 | tf_op jit(solution)/shard_map/dot_general | solution.py:56
  31.7 2.6 %scatter_custom_fusion.1 = bf16[1024,512]{1,0:T(8,128)(2,1)} fusion(s32[256]{0:T(256)S(1)} %bitcast.86, bf16[256,512]{1,0:T(8,128)(2,1)S(1)} %fusion.19, bf16[]{:T(256)} %constant.35.clone.1), kind=kCustom, calls=%fused_computation.60 | custom fusion | bytes 1048578 | tf_op jit(solution)/shard_map/scatter | solution.py:80
  34.4 6.0 %all-to-all-start.1 = ((bf16[8,128,512]{2,1,0:T(8,128)(2,1)}), bf16[8,128,512]{2,1,0:T(8,128)(2,1)S(1)}, u32[]{:S(2)}, u32[]{:S(2)}) async-start(bf16[8,128,512]{2,1,0:T(8,128)(2,1)} %bitcast.22), calls=%async_computation.1 | async-start | bytes 2097152 | tf_op jit(solution)/shard_map/all_to_all | solution.py:84
  40.6 4.4 %multiply_convert_fusion = (bf16[512,512]{1,0:T(8,128)(2,1)S(1)}, bf16[512,512]{1,0:T(8,128)(2,1)S(1)}) fusion(), kind=kLoop, calls=%fused_computation.36 | loop fusion | flops 4718592 | bytes 1048576 | tf_op jit(solution)/shard_map/convert_element_type | solution.py:16
  45.0 20.8 %all-to-all-done.1 = bf16[8,128,512]{2,1,0:T(8,128)(2,1)S(1)} async-done(((bf16[8,128,512]{2,1,0:T(8,128)(2,1)}), bf16[8,128,512]{2,1,0:T(8,128)(2,1)S(1)}, u32[]{:S(2)}, u32[]{:S(2)}) %all-to-all-start.1) | async-done | bytes 1048608 | tf_op jit(solution)/shard_map/all_to_all | solution.py:84
  65.8 1.3 fusion.13
  67.0 0.5 copy.29
  67.6 4.4 %reshape.157 = bf16[32,32,2,16,16]{1,0,4,3,2:T(8,128)(2,1)} reshape(bf16[1024,512]{0,1:T(8,128)(2,1)S(1)} %copy.29) | data formatting | bytes 2097152 | tf_op jit(solution)/shard_map/reshape | solution.py:106
  72.0 8.8 %copy.30 = bf16[2,32,16,32,16]{4,3,2,1,0:T(8,128)(2,1)} copy(bf16[2,32,16,32,16]{3,1,4,2,0:T(8,128)(2,1)} %bitcast.69) | data formatting | bytes 2097152 | tf_op jit(solution)/shard_map/transpose | solution.py:107
  80.7 14.4 %reshape.158 = bf16[1024,512]{1,0:T(8,128)(2,1)S(1)} reshape(bf16[2,32,16,32,16]{4,3,2,1,0:T(8,128)(2,1)} %copy.30) | data formatting | bytes 2097152 | tf_op jit(solution)/shard_map/reshape | solution.py:108
  95.2 1.2 fusion.32
  96.4 0.4 fusion.37
  96.9 1.0 copy.31
  97.9 1.2 copy.37
  99.2 23.7 %reduce-scatter.4.cloned.1.call-done = bf16[128,1024]{1,0:T(8,128)(2,1)} async-done(((bf16[512,1024]{1,0:T(8,128)(2,1)}), bf16[128,1024]{1,0:T(8,128)(2,1)}) %reduce-scatter.4.cloned.1.call-update) | async-done | bytes 262160
  122.9 1.1 reshape.178
  124.0 0.4 fusion.62
  124.8 1.1 convolution_bitcast_fusion
  (23 shorter events, 1.8 us)
Async XLA Ops:
  11.6 22.7 %all-to-all-start = ((s32[8,1,128]{2,1,0:T(1,128)}), s32[8,1,128]{2,1,0:T(1,128)S(1)}, u32[]{:S(2)}, u32[]{:S(2)}) async-start(s32[8,1,128]{2,1,0:T(1,128)} %bitcast.8), calls=%async_computation | async-start | bytes 8192 | tf_op jit(solution)/shard_map/all_to_all | solution.py:91
  19.6 3.5 %copy-start = (bf16[8,2,512,256]{3,2,1,0:T(8,128)(2,1)S(1)}, bf16[8,2,512,256]{3,2,1,0:T(8,128)(2,1)}, u32[]{:S(2)}) copy-start(bf16[8,2,512,256]{3,2,1,0:T(8,128)(2,1)} %param.12) | copy-start | bytes 12582916
  23.1 0.7 copy-start.4
  23.1 1.1 copy-start.1
  23.7 1.1 copy-start.2
  23.8 1.2 copy-start.3
  34.4 31.4 %all-to-all-start.1 = ((bf16[8,128,512]{2,1,0:T(8,128)(2,1)}), bf16[8,128,512]{2,1,0:T(8,128)(2,1)S(1)}, u32[]{:S(2)}, u32[]{:S(2)}) async-start(bf16[8,128,512]{2,1,0:T(8,128)(2,1)} %bitcast.22), calls=%async_computation.1 | async-start | bytes 2097152 | tf_op jit(solution)/shard_map/all_to_all | solution.py:84
  40.4 82.5 %reduce-scatter.4.cloned.1.call-start = ((), (), s32[]{:S(2)}) async-start(), calls=%async_computation.3 | async-start | bytes 1310720
Sparse Core Ops, SparseCore 0:
  99.3 23.5 reduce-scatter.3
where the time goes:
time: 133 us
  waiting for transfers between devices  44.5 us (33%)
  local copies, waits for them, and re-layouts  42 us (32%)
  between operations  13.6 us (10%)
  starting transfers between devices  13.5 us (10%)
  other arithmetic  13.2 us (10%)
  matrix products  5.96 us (4%)
    unnamed x2, waiting for transfers between devices  23.7 us
    all_to_all x1, waiting for transfers between devices, shards(): lax.all_to_all(patch_buffer.reshape(peer_count, capacity, -1), 'facet', s...  20.8 us
    reshape x1, local copies, waits for them, and re-layouts, shards(): uv_grid = blocks.reshape(nblocks, nblocks, 2, PSIDE, PSIDE).transpose(2,...  14.4 us
    transpose x1, local copies, waits for them, and re-layouts, shards(): uv_grid = blocks.reshape(nblocks, nblocks, 2, PSIDE, PSIDE).transpose(2,...  8.76 us
    all_to_all x1, starting transfers between devices, shards(): lax.all_to_all(cell_buffer.reshape(peer_count, capacity), 'facet', split_...  7.31 us
    all_to_all x1, starting transfers between devices, shards(): lax.all_to_all(patch_buffer.reshape(peer_count, capacity, -1), 'facet', s...  6 us
    unnamed x16, local copies, waits for them, and re-layouts  5.82 us
    reshape x1, local copies, waits for them, and re-layouts, shards(): blocks.reshape(nblocks, nblocks, 2, PSIDE, PSIDE).transpose(2, 0, 3, 1, 4)  4.4 us
  transfers between devices with their start and end apart: 3, of which 2 were waited for; matrix products, arithmetic and copies ran while one was open for 13% of the time, Pallas kernels for 0%

commit v1 on v0

--- a/solution.py
+++ b/solution.py
@@ -1,10 +1,53 @@
+import functools
+
 import jax
 import jax.numpy as jnp
+import numpy as np
 from jax import lax
+from jax.experimental import pallas as pl
+from jax.experimental.pallas import tpu as pltpu
 from jax.sharding import PartitionSpec as P
 
 GRID = 512
 PSIDE = 16
+NBLK = GRID // PSIDE
+LANES = 128
+SUBLANES = 8
+
+SIN_POLY = (6.283185280261414, -41.34168066806301, 81.602480742862, -76.58128455932604, 39.76072207590882)
+COS_POLY = (
+    0.999999999779904,
+    -19.739208548314995,
+    64.93934655286789,
+    -85.45356819388616,
+    60.14395231405798,
+    -24.98183599569851,
+)
+
+
+def horner(square, coefficients):
+    value = jnp.full_like(square, coefficients[-1])
+    for coefficient in coefficients[-2::-1]:
+        value = value * square + coefficient
+    return value
+
+
+def cos_sin_turns(turns):
+    halves = jnp.round(turns * 2.0)
+    rest = turns - halves * 0.5
+    half = halves * 0.5
+    sign = 1.0 - 4.0 * (half - jnp.floor(half))
+    square = rest * rest
+    return (horner(square, COS_POLY) * sign, rest * horner(square, SIN_POLY) * sign)
+
+
+def compiler_params(mebibytes):
+    return pltpu.CompilerParams(vmem_limit_bytes=mebibytes << 20)
+
+
+VMEM = pl.BlockSpec(memory_space=pltpu.VMEM)
+SMEM = pl.BlockSpec(memory_space=pltpu.SMEM)
+ANY = pl.BlockSpec(memory_space=pl.ANY)
 
 
 def dft_tables(length):
@@ -124,6 +167,228 @@
     return facet_image[None]
 
 
+def gather_kernel(peers, capacity, me_ref, centers_ref, facet_ref, plane_ref, cell_ref, vis_ref, uvw_ref, kern_ref, *rest):
+    out_refs, (kern_buf, rows_buf, kern_sem) = rest[:peers], rest[peers:]
+    planes, _, depth, cells = kern_ref.shape
+    tiles = facet_ref.shape[1]
+    copies = [pltpu.make_async_copy(kern_ref.at[p], kern_buf.at[p], kern_sem.at[p]) for p in range(planes)]
+    for copy in copies:
+        copy.start()
+    facet = facet_ref[...]
+    l_row = jnp.zeros(facet.shape, jnp.float32)
+    m_row = jnp.zeros(facet.shape, jnp.float32)
+    for f in range(peers):
+        hit = facet == f
+        l_row = jnp.where(hit, centers_ref[f, 0], l_row)
+        m_row = jnp.where(hit, centers_ref[f, 1], m_row)
+    d_row = jnp.sqrt(1.0 - l_row * l_row - m_row * m_row) - 1.0
+    plane_row = plane_ref[...].astype(jnp.float32)
+    zero_row = jnp.zeros_like(l_row)
+    columns = jnp.concatenate([l_row, m_row, d_row, plane_row] + [zero_row] * 4, axis=0).T
+    l_col, m_col, d_col, plane_col = (columns[:, i : i + 1] for i in range(4))
+
+    u = uvw_ref[0].astype(jnp.float32)
+    v = uvw_ref[1].astype(jnp.float32)
+    w = uvw_ref[2].astype(jnp.float32)
+    cosine, sine = cos_sin_turns(l_col * u + m_col * v + d_col * w)
+    real = vis_ref[:, 0, :].astype(jnp.float32)
+    imag = vis_ref[:, 1, :].astype(jnp.float32)
+    rot_real = (real * cosine + imag * sine).astype(jnp.bfloat16)
+    rot_imag = (imag * cosine - real * sine).astype(jnp.bfloat16)
+    rows_buf[:tiles, :depth] = rot_real
+    rows_buf[:tiles, depth:] = -rot_imag
+    rows_buf[tiles:, :depth] = rot_imag
+    rows_buf[tiles:, depth:] = rot_real
+
+    relative = facet ^ me_ref[0]
+    lanes = lax.broadcasted_iota(jnp.int32, (tiles, tiles), 1)
+    earlier = (lax.broadcasted_iota(jnp.int32, (tiles, tiles), 0) < lanes).astype(jnp.float32).astype(jnp.bfloat16)
+    hits = lax.broadcasted_iota(jnp.int32, (peers, tiles), 0) == relative
+    before = jnp.dot(hits.astype(jnp.float32).astype(jnp.bfloat16), earlier, preferred_element_type=jnp.float32)
+    rank = jnp.sum(jnp.where(hits, before, 0.0), axis=0, keepdims=True)
+    slot = relative * capacity + rank.astype(jnp.int32)
+    slots = peers * capacity
+    placing = lax.broadcasted_iota(jnp.int32, (slots, tiles), 0) == slot
+    placing = placing.astype(jnp.float32).astype(jnp.bfloat16)
+
+    total = jnp.zeros((2 * tiles, cells), jnp.float32)
+    plane_two = jnp.concatenate([plane_col, plane_col], axis=0)
+    for p in range(planes):
+        mask = (plane_two == float(p)).astype(jnp.float32).astype(jnp.bfloat16)
+        copies[p].wait()
+        total = total + jnp.dot(
+            rows_buf[...] * mask, kern_buf[p].reshape(2 * depth, cells), preferred_element_type=jnp.float32
+        )
+    patches = jnp.concatenate([total[:tiles], total[tiles:]], axis=1).astype(jnp.bfloat16)
+    placed = jnp.dot(placing, patches, preferred_element_type=jnp.float32).astype(jnp.bfloat16)
+    cell = cell_ref[...].astype(jnp.float32)
+    block_u = jnp.floor(cell * (1.0 / NBLK))
+    block_v = cell - block_u * NBLK
+    pair = jnp.concatenate([block_u, block_v] + [zero_row] * (SUBLANES - 2), axis=0).astype(jnp.bfloat16)
+    pair = lax.dot_general(pair, placing, (((1,), (1,)), ((), ())), preferred_element_type=jnp.float32)
+    pair = pair.astype(jnp.bfloat16)
+    for s in range(peers):
+        rows = slice(s * capacity, (s + 1) * capacity)
+        for j in range(2 * cells // LANES):
+            out_refs[s][j * capacity : (j + 1) * capacity, :] = placed[rows, j * LANES : (j + 1) * LANES]
+        out_refs[s][2 * cells // LANES * capacity :, :] = pair[:, rows]
+
+
+def image_kernel(peers, groups, capacity, me_ref, table_ref, *rest):
+    in_refs, out_refs = rest[:peers], rest[peers : peers + groups]
+    phases_buf, patch_buf, table_buf = rest[peers + groups :]
+    cells = PSIDE * PSIDE
+    slots = peers * capacity
+    share = cells // groups
+    half_tiles = cells // LANES
+    for s in range(peers):
+        rows = slice(s * capacity, (s + 1) * capacity)
+        below = slice(slots + s * capacity, slots + (s + 1) * capacity)
+        for j in range(half_tiles):
+            left = slice(j * LANES, (j + 1) * LANES)
+            right = slice(cells + j * LANES, cells + (j + 1) * LANES)
+            real = in_refs[s][j * capacity : (j + 1) * capacity, :]
+            imag = in_refs[s][(half_tiles + j) * capacity : (half_tiles + j + 1) * capacity, :]
+            patch_buf[rows, left] = real
+            patch_buf[rows, right] = imag
+            patch_buf[below, left] = -imag
+            patch_buf[below, right] = real
+    for s in range(groups):
+        start = pl.multiple_of((me_ref[0] ^ s) * share, share)
+        table_buf[s * share : (s + 1) * share, :] = table_ref[pl.ds(start, share), :]
+
+    first = 2 * half_tiles * capacity
+    block_u = jnp.concatenate([ref[first : first + SUBLANES, :][0:1].astype(jnp.float32) for ref in in_refs], axis=1)
+    block_v = jnp.concatenate([ref[first : first + SUBLANES, :][1:2].astype(jnp.float32) for ref in in_refs], axis=1)
+    index = lax.broadcasted_iota(jnp.int32, (NBLK, slots), 0).astype(jnp.float32)
+    cos_u, sin_u = cos_sin_turns(index * block_u * (1.0 / NBLK))
+    cos_v, sin_v = cos_sin_turns(index * block_v * (1.0 / NBLK))
+
+    lane = lax.broadcasted_iota(jnp.int32, (NBLK, cells), 1)
+    row = lax.broadcasted_iota(jnp.int32, (NBLK, cells), 0)
+    patch_u, patch_v = lane // PSIDE, lane % PSIDE
+    twid_u = cos_sin_turns((row * patch_u).astype(jnp.float32) * (1.0 / GRID))
+    twid_v = cos_sin_turns((row * patch_v).astype(jnp.float32) * (1.0 / GRID))
+
+    per_chunk = 8
+    for chunk in range(NBLK // per_chunk):
+        for i in range(per_chunk):
+            j = chunk * per_chunk + i
+            cu, su = cos_u[j : j + 1], sin_u[j : j + 1]
+            rows = slice(i * NBLK, (i + 1) * NBLK)
+            buf = phases_buf.at[chunk % 2]
+            buf[rows, :slots] = (cu * cos_v - su * sin_v).astype(jnp.bfloat16)
+            buf[rows, slots:] = (cu * sin_v + su * cos_v).astype(jnp.bfloat16)
+        spectrum = jnp.dot(phases_buf[chunk % 2], patch_buf[...], preferred_element_type=jnp.float32)
+        turned = []
+        for i in range(per_chunk):
+            j = chunk * per_chunk + i
+            rows = slice(i * NBLK, (i + 1) * NBLK)
+            real, imag = spectrum[rows, :cells], spectrum[rows, cells:]
+            tr = twid_u[0][j : j + 1] * twid_v[0] - twid_u[1][j : j + 1] * twid_v[1]
+            ti = twid_u[0][j : j + 1] * twid_v[1] + twid_u[1][j : j + 1] * twid_v[0]
+            turned.append(jnp.concatenate([real * tr - imag * ti, real * ti + imag * tr], axis=1).astype(jnp.bfloat16))
+        turned = jnp.concatenate(turned, axis=0)
+        image = lax.dot_general(
+            table_buf[...], turned, (((1,), (1,)), ((), ())), preferred_element_type=jnp.float32
+        ).astype(jnp.bfloat16)
+        width = per_chunk * NBLK
+        for s in range(groups):
+            out_refs[s][:, chunk * width : (chunk + 1) * width] = image[s * share : (s + 1) * share]
+
+
+def finish_kernel(groups, *refs):
+    in_refs, out_ref = refs[:groups], refs[groups]
+    columns = PSIDE // groups
+    per_tile = LANES // NBLK
+    lane = lax.broadcasted_iota(jnp.int32, (PSIDE, LANES), 1) // NBLK
+    for tile in range(NBLK // per_tile):
+        lanes = slice(tile * LANES, (tile + 1) * LANES)
+        total = in_refs[0][:, lanes].astype(jnp.float32)
+        for ref in in_refs[1:]:
+            total = total + ref[:, lanes].astype(jnp.float32)
+        for i in range(per_tile):
+            value = jnp.zeros((PSIDE, LANES), jnp.float32)
+            for kq in range(columns):
+                piece = total[kq * PSIDE : (kq + 1) * PSIDE]
+                shift = (kq - i) * NBLK % LANES
+                piece = pltpu.roll(piece, shift, 1) if shift else piece
+                value = jnp.where(lane == kq, piece, value)
+            out_ref[pl.ds(tile * per_tile + i, PSIDE, stride=NBLK), :] = value
+
+
+def patch_table(groups):
+    index = np.arange(PSIDE)
+    kq, jq = (a.reshape(-1, 1) for a in np.meshgrid(index, index, indexing="ij"))
+    pu, pv = (a.reshape(1, -1) for a in np.meshgrid(index, index, indexing="ij"))
+    angle = 2.0 * np.pi * ((pu * jq + pv * kq) % PSIDE) / PSIDE
+    return np.concatenate([np.cos(angle), -np.sin(angle)], axis=1) / GRID
+
+
+def swap(piece, axis, distance):
+    count = lax.axis_size(axis)
+    return lax.ppermute(piece, axis, [(i, i ^ distance) for i in range(count)])
+
+
+def packed_shards(visibilities, uvw, facet_of, plane_of, cell_of, kernels, centers):
+    peers, groups = lax.axis_size("facet"), lax.axis_size("freq")
+    tiles = visibilities.shape[1]
+    capacity = 4 * tiles // peers
+    planes, _, depth, cells = kernels.shape
+    payload = jax.ShapeDtypeStruct((2 * cells // LANES * capacity + SUBLANES, LANES), jnp.bfloat16)
+    facet_index = lax.axis_index("facet").reshape(1).astype(jnp.int32)
+    group_index = lax.axis_index("freq").reshape(1).astype(jnp.int32)
+    pieces = pl.pallas_call(
+        functools.partial(gather_kernel, peers, capacity),
+        out_shape=[payload] * peers,
+        in_specs=[SMEM, SMEM, VMEM, VMEM, VMEM, VMEM, VMEM, ANY],
+        out_specs=[VMEM] * peers,
+        scratch_shapes=[
+            pltpu.VMEM(kernels.shape, jnp.bfloat16),
+            pltpu.VMEM((2 * tiles, 2 * depth), jnp.bfloat16),
+            pltpu.SemaphoreType.DMA((planes,)),
+        ],
+        compiler_params=compiler_params(40),
+        name="gather",
+    )(
+        facet_index,
+        centers,
+        facet_of.reshape(1, tiles),
+        plane_of,
+        cell_of,
+        visibilities[0],
+        uvw[0].transpose(1, 0, 2),
+        kernels,
+    )
+    received = [pieces[0]] + [swap(pieces[s], "facet", s) for s in range(1, peers)]
+    share = cells // groups
+    image = jax.ShapeDtypeStruct((share, NBLK * NBLK), jnp.bfloat16)
+    slots = peers * capacity
+    images = pl.pallas_call(
+        functools.partial(image_kernel, peers, groups, capacity),
+        out_shape=[image] * groups,
+        in_specs=[SMEM] + [VMEM] * (1 + peers),
+        out_specs=[VMEM] * groups,
+        scratch_shapes=[
+            pltpu.VMEM((2, 8 * NBLK, 2 * slots), jnp.bfloat16),
+            pltpu.VMEM((2 * slots, 2 * cells), jnp.bfloat16),
+            pltpu.VMEM((cells, 2 * cells), jnp.bfloat16),
+        ],
+        compiler_params=compiler_params(40),
+        name="image",
+    )(group_index, jnp.asarray(patch_table(groups), jnp.bfloat16), *received)
+    summed = [images[0]] + [swap(images[s], "freq", s) for s in range(1, groups)]
+    facet_image = pl.pallas_call(
+        functools.partial(finish_kernel, groups),
+        out_shape=jax.ShapeDtypeStruct((GRID, GRID // groups), jnp.float32),
+        in_specs=[VMEM] * groups,
+        out_specs=VMEM,
+        compiler_params=compiler_params(16),
+        name="finish",
+    )(*summed)
+    return facet_image[None]
+
+
 def solution(mesh):
     in_specs = (
         P("freq", "facet", None, None),
@@ -135,4 +400,12 @@
         P(),
     )
     out_specs = P("facet", None, "freq")
-    return jax.shard_map(shards, mesh=mesh, in_specs=in_specs, out_specs=out_specs, check_vma=False)
+
+    def body(*args):
+        peers, groups = lax.axis_size("facet"), lax.axis_size("freq")
+        capacity = 4 * args[0].shape[1] // peers
+        powers = peers & (peers - 1) == 0 and groups & (groups - 1) == 0
+        packed = capacity % LANES == 0 and powers and GRID // groups == LANES
+        return (packed_shards if packed else shards)(*args)
+
+    return jax.shard_map(body, mesh=mesh, in_specs=in_specs, out_specs=out_specs, check_vma=False)

time: 133 us -> 59.2 us (0.45)
  the two profiles are of different devices: /device:TPU:0 before, /device:TPU:19 now
where the time goes in v1:
time: 59.2 us; the launch traced here: 58.9 us
  waiting for transfers between devices  27.7 us (47%)
  Pallas kernels  13 us (22%)
  starting transfers between devices  11 us (19%)
  local copies, waits for them, and re-layouts  7.15 us (12%)
    ppermute x10, waiting for transfers between devices, swap(): return lax.ppermute(piece, axis, [(i, i ^ distance) for i in range(count)])  27.7 us
    ppermute x10, starting transfers between devices, swap(): return lax.ppermute(piece, axis, [(i, i ^ distance) for i in range(count)])  11 us
    pallas_call x1, Pallas kernels, packed_shards(): pl.pallas_call(functools.partial(gather_kernel, peers, capacity), out_sha...  8.18 us
    unnamed x15, local copies, waits for them, and re-layouts  7.15 us
    pallas_call x1, Pallas kernels, packed_shards(): pl.pallas_call(functools.partial(image_kernel, peers, groups, capacity),...  3.79 us
  transfers between devices with their start and end apart: 10, of which 7 were waited for; matrix products, arithmetic and copies ran while one was open for 0% of the time, Pallas kernels for 0%

profile of v1, /device:TPU:19, one launch (start us, length us, event | category | flops | bytes accessed | tf_op | source)
XLA Modules:
  0.0 58.9 jit_solution(10928976161605886971)
XLA Ops:
  0.0 0.8 %copy.9.centers_ref = f32[8,2]{1,0:T(8,128)S(1)} copy(f32[8,2]{0,1:T(2,128)} %param.14) | data formatting | bytes 128 | tf_op args[6]
  0.8 0.0 copy-start
  0.8 2.2 %copy-done = bf16[8,2,512,256]{3,2,1,0:T(8,128)(2,1)S(1)} copy-done((bf16[8,2,512,256]{3,2,1,0:T(8,128)(2,1)S(1)}, bf16[8,2,512,256]{3,2,1,0:T(8,128)(2,1)}, u32[]{:S(2)}) %copy-start) | copy-done | bytes 4194328
  2.9 1.1 %copy-done.1 = bf16[1,256,3,512]{3,1,2,0:T(8,128)(2,1)S(1)} copy-done((bf16[1,256,3,512]{3,1,2,0:T(8,128)(2,1)S(1)}, bf16[1,256,3,512]{3,1,2,0:T(8,128)(2,1)}, u32[]{:S(2)}) %copy-start.1) | copy-done | bytes 786456
  4.1 1.0 %copy-done.2 = bf16[1,256,2,512]{3,2,1,0:T(2,128)(2,1)S(1)} copy-done((bf16[1,256,2,512]{3,2,1,0:T(2,128)(2,1)S(1)}, bf16[1,256,2,512]{3,2,1,0:T(2,128)(2,1)}, u32[]{:S(2)}) %copy-start.2) | copy-done | bytes 524312
  5.1 0.7 %copy-done.4 = s32[1,256,1]{1,2,0:T(1,128)S(1)} copy-done((s32[1,256,1]{1,2,0:T(1,128)S(1)}, s32[1,256,1]{1,2,0:T(1,128)}, u32[]{:S(2)}) %copy-start.4) | copy-done | bytes 1048
  5.8 0.7 %copy-done.5 = s32[1,256]{1,0:T(1,128)S(1)} copy-done((s32[1,256]{1,0:T(1,128)S(1)}, s32[1,256]{1,0:T(1,128)}, u32[]{:S(2)}) %copy-start.5) | copy-done | bytes 1048
  6.5 0.7 %copy-done.6 = s32[1,256]{1,0:T(1,128)S(1)} copy-done((s32[1,256]{1,0:T(1,128)S(1)}, s32[1,256]{1,0:T(1,128)}, u32[]{:S(2)}) %copy-start.6) | copy-done | bytes 1048
  7.2 8.2 %gather.1 = (bf16[520,128]{1,0:T(8,128)(2,1)S(1)}, bf16[520,128]{1,0:T(8,128)(2,1)S(1)}, bf16[520,128]{1,0:T(8,128)(2,1)S(1)}, bf16[520,128]{1,0:T(8,128)(2,1)S(...) custom-call(s32[1]{0:T(128)} %bitcast.1.me_ref, ...), custom_call_target="tpu_custom_call" | custom-call | tf_op jit(solution)/shard_map/gather/pallas_call | solution.py:341
  15.3 1.3 %collective-permute-start = (bf16[520,128]{1,0:T(8,128)(2,1)S(1)}, bf16[520,128]{1,0:T(8,128)(2,1)S(1)}, u32[]{:S(2)}, u32[]{:S(2)}) collective-permute-start(bf16[520,128]{1,0:T(8,128)(2,1)S(1)} %get-tuple-element.18), channel_id=1, source_target_pairs={{0,4},{4,0},{8,12},{12,8},{16,20},{20,16},{24,28},{28,24},{1,5},{5... | collective-permute-start | bytes 399368 | tf_op jit(solution)/shard_map/ppermute | solution.py:330
  16.7 1.3 %collective-permute-start.1 = (bf16[520,128]{1,0:T(8,128)(2,1)S(1)}, bf16[520,128]{1,0:T(8,128)(2,1)S(1)}, u32[]{:S(2)}, u32[]{:S(2)}) collective-permute-start(bf16[520,128]{1,0:T(8,128)(2,1)S(1)} %get-tuple-element.19), channel_id=1, source_target_pairs={{0,8},{4,12},{8,0},{12,4},{16,24},{20,28},{24,16},{28,20},{1,9},{5... | collective-permute-start | bytes 399368 | tf_op jit(solution)/shard_map/ppermute | solution.py:330
  17.9 0.1 collective-permute-start.2
  18.1 0.1 collective-permute-start.3
  18.1 3.3 %collective-permute-start.4 = (bf16[520,128]{1,0:T(8,128)(2,1)S(1)}, bf16[520,128]{1,0:T(8,128)(2,1)S(1)}, u32[]{:S(2)}, u32[]{:S(2)}) collective-permute-start(bf16[520,128]{1,0:T(8,128)(2,1)S(1)} %get-tuple-element.22), channel_id=1, source_target_pairs={{0,20},{4,16},{8,28},{12,24},{16,4},{20,0},{24,12},{28,8},{1,21},{... | collective-permute-start | bytes 399368 | tf_op jit(solution)/shard_map/ppermute | solution.py:330
  21.4 0.0 collective-permute-done.rest_1_
  21.4 0.2 collective-permute-start.5
  21.6 0.0 collective-permute-done.1.rest_2_
  21.6 1.2 %collective-permute-start.6 = (bf16[520,128]{1,0:T(8,128)(2,1)S(1)}, bf16[520,128]{1,0:T(8,128)(2,1)S(1)}, u32[]{:S(2)}, u32[]{:S(2)}) collective-permute-start(bf16[520,128]{1,0:T(8,128)(2,1)S(1)} %get-tuple-element.24), channel_id=1, source_target_pairs={{0,28},{4,24},{8,20},{12,16},{16,12},{20,8},{24,4},{28,0},{1,29},{... | collective-permute-start | bytes 399368 | tf_op jit(solution)/shard_map/ppermute | solution.py:330
  22.8 3.0 %collective-permute-done.2.rest_3_ = bf16[520,128]{1,0:T(8,128)(2,1)S(1)} collective-permute-done((bf16[520,128]{1,0:T(8,128)(2,1)S(1)}, bf16[520,128]{1,0:T(8,128)(2,1)S(1)}, u32[]{:S(2)}, u32[]{:S(2)}) %collective-permute-start.2) | collective-permute-done | bytes 133152 | tf_op jit(solution)/shard_map/ppermute | solution.py:330
  25.8 0.6 collective-permute-done.3.rest_4_
  26.4 2.8 %collective-permute-done.4.rest_5_ = bf16[520,128]{1,0:T(8,128)(2,1)S(1)} collective-permute-done((bf16[520,128]{1,0:T(8,128)(2,1)S(1)}, bf16[520,128]{1,0:T(8,128)(2,1)S(1)}, u32[]{:S(2)}, u32[]{:S(2)}) %collective-permute-start.4) | collective-permute-done | bytes 133152 | tf_op jit(solution)/shard_map/ppermute | solution.py:330
  29.2 10.4 %collective-permute-done.5.rest_6_ = bf16[520,128]{1,0:T(8,128)(2,1)S(1)} collective-permute-done((bf16[520,128]{1,0:T(8,128)(2,1)S(1)}, bf16[520,128]{1,0:T(8,128)(2,1)S(1)}, u32[]{:S(2)}, u32[]{:S(2)}) %collective-permute-start.5) | collective-permute-done | bytes 133152 | tf_op jit(solution)/shard_map/ppermute | solution.py:330
  39.7 4.5 %collective-permute-done.6.rest_7_ = bf16[520,128]{1,0:T(8,128)(2,1)S(1)} collective-permute-done((bf16[520,128]{1,0:T(8,128)(2,1)S(1)}, bf16[520,128]{1,0:T(8,128)(2,1)S(1)}, u32[]{:S(2)}, u32[]{:S(2)}) %collective-permute-start.6) | collective-permute-done | bytes 133152 | tf_op jit(solution)/shard_map/ppermute | solution.py:330
  44.2 0.0 copy-done.3
  44.2 3.8 %image.1 = (bf16[64,1024]{1,0:T(8,128)(2,1)S(1)}, bf16[64,1024]{1,0:T(8,128)(2,1)S(1)}, bf16[64,1024]{1,0:T(8,128)(2,1)S(1)}, bf16[64,1024]{1,0:T(8,128)(2,1)S(1)}) custom-call(s32[1]{0:T(128)} %bitcast.me_ref, bf16[256,512]{1,0:T(8,128)(2,1)S(1)} %copy-done.3, bf16[520,128]{1,0:T(8,128)(2,1)S(1)} %get-tuple-element.17.rest_0_, ...), custom_call_target="tpu_custom_call" | custom-call | tf_op jit(solution)/shard_map/image/pallas_call | solution.py:367
  48.0 1.8 %collective-permute-start.7 = (bf16[64,1024]{1,0:T(8,128)(2,1)S(1)}, bf16[64,1024]{1,0:T(8,128)(2,1)S(1)}, u32[]{:S(2)}, u32[]{:S(2)}) collective-permute-start(bf16[64,1024]{1,0:T(8,128)(2,1)S(1)} %get-tuple-element.26), channel_id=1, source_target_pairs={{0,1},{1,0},{2,3},{3,2},{4,5},{5,4},{6,7},{7,6},{8,9},{9,8},{10,11... | collective-permute-start | bytes 393224 | tf_op jit(solution)/shard_map/ppermute | solution.py:330
  49.8 0.3 collective-permute-start.8
  50.1 1.5 %collective-permute-start.9 = (bf16[64,1024]{1,0:T(8,128)(2,1)S(1)}, bf16[64,1024]{1,0:T(8,128)(2,1)S(1)}, u32[]{:S(2)}, u32[]{:S(2)}) collective-permute-start(bf16[64,1024]{1,0:T(8,128)(2,1)S(1)} %get-tuple-element.28), channel_id=1, source_target_pairs={{0,3},{1,2},{2,1},{3,0},{4,7},{5,6},{6,5},{7,4},{8,11},{9,10},{10,... | collective-permute-start | bytes 393224 | tf_op jit(solution)/shard_map/ppermute | solution.py:330
  51.5 0.0 collective-permute-done.7.refs_1_
  51.5 3.3 %collective-permute-done.8.refs_2_ = bf16[64,1024]{1,0:T(8,128)(2,1)S(1)} collective-permute-done((bf16[64,1024]{1,0:T(8,128)(2,1)S(1)}, bf16[64,1024]{1,0:T(8,128)(2,1)S(1)}, u32[]{:S(2)}, u32[]{:S(2)}) %collective-permute-start.8) | collective-permute-done | bytes 131104 | tf_op jit(solution)/shard_map/ppermute | solution.py:330
  54.8 3.1 %collective-permute-done.9.refs_3_ = bf16[64,1024]{1,0:T(8,128)(2,1)S(1)} collective-permute-done((bf16[64,1024]{1,0:T(8,128)(2,1)S(1)}, bf16[64,1024]{1,0:T(8,128)(2,1)S(1)}, u32[]{:S(2)}, u32[]{:S(2)}) %collective-permute-start.9) | collective-permute-done | bytes 131104 | tf_op jit(solution)/shard_map/ppermute | solution.py:330
  57.9 1.1 %finish.1 = f32[512,128]{1,0:T(8,128)} custom-call(bf16[64,1024]{1,0:T(8,128)(2,1)S(1)} %get-tuple-element.25.refs_0_, bf16[64,1024]{1,0:T(8,128)(2,1)S(1)} %collective-permute-done.7.refs_1_, bf16[64,1024]{1,0:T(8,128)(2,1)S(1)} %collective-permute-done.8.refs_2_, bf16[64,1024]{1,0:T(8,128)(2,1)S(1)} %collective-permute-done.9.refs_3_), custom_call_target="tpu_custom_call" | custom-call | tf_op jit(solution)/shard_map/finish/pallas_call | solution.py:381
  (6 shorter events, 0.0 us)
Async XLA Ops:
  0.8 2.2 %copy-start = (bf16[8,2,512,256]{3,2,1,0:T(8,128)(2,1)S(1)}, bf16[8,2,512,256]{3,2,1,0:T(8,128)(2,1)}, u32[]{:S(2)}) copy-start(bf16[8,2,512,256]{3,2,1,0:T(8,128)(2,1)} %kern_ref.1) | copy-start | bytes 12582916
  2.9 1.1 %copy-start.1 = (bf16[1,256,3,512]{3,1,2,0:T(8,128)(2,1)S(1)}, bf16[1,256,3,512]{3,1,2,0:T(8,128)(2,1)}, u32[]{:S(2)}) copy-start(bf16[1,256,3,512]{3,1,2,0:T(8,128)(2,1)} %param.9) | copy-start | bytes 2359300
  4.1 1.0 %copy-start.2 = (bf16[1,256,2,512]{3,2,1,0:T(2,128)(2,1)S(1)}, bf16[1,256,2,512]{3,2,1,0:T(2,128)(2,1)}, u32[]{:S(2)}) copy-start(bf16[1,256,2,512]{3,2,1,0:T(2,128)(2,1)} %param.8) | copy-start | bytes 1572868
  5.1 0.7 %copy-start.4 = (s32[1,256,1]{1,2,0:T(1,128)S(1)}, s32[1,256,1]{1,2,0:T(1,128)}, u32[]{:S(2)}) copy-start(s32[1,256,1]{1,2,0:T(1,128)} %param.10) | copy-start | bytes 3076
  5.8 0.7 %copy-start.5 = (s32[1,256]{1,0:T(1,128)S(1)}, s32[1,256]{1,0:T(1,128)}, u32[]{:S(2)}) copy-start(s32[1,256]{1,0:T(1,128)} %plane_ref.1) | copy-start | bytes 3076
  6.5 0.7 %copy-start.6 = (s32[1,256]{1,0:T(1,128)S(1)}, s32[1,256]{1,0:T(1,128)}, u32[]{:S(2)}) copy-start(s32[1,256]{1,0:T(1,128)} %cell_ref.1) | copy-start | bytes 3076
  7.2 37.0 %copy-start.3 = (bf16[256,512]{1,0:T(8,128)(2,1)S(1)}, bf16[256,512]{1,0:T(8,128)(2,1)}, u32[]{:S(2)}) copy-start(bf16[256,512]{1,0:T(8,128)(2,1)} %constant.11.clone.table_ref) | copy-start | bytes 786436
  15.3 6.0 %collective-permute-start = (bf16[520,128]{1,0:T(8,128)(2,1)S(1)}, bf16[520,128]{1,0:T(8,128)(2,1)S(1)}, u32[]{:S(2)}, u32[]{:S(2)}) collective-permute-start(bf16[520,128]{1,0:T(8,128)(2,1)S(1)} %get-tuple-element.18), channel_id=1, source_target_pairs={{0,4},{4,0},{8,12},{12,8},{16,20},{20,16},{24,28},{28,24},{1,5},{5... | collective-permute-start | bytes 399368 | tf_op jit(solution)/shard_map/ppermute | solution.py:330
  16.7 4.9 %collective-permute-start.1 = (bf16[520,128]{1,0:T(8,128)(2,1)S(1)}, bf16[520,128]{1,0:T(8,128)(2,1)S(1)}, u32[]{:S(2)}, u32[]{:S(2)}) collective-permute-start(bf16[520,128]{1,0:T(8,128)(2,1)S(1)} %get-tuple-element.19), channel_id=1, source_target_pairs={{0,8},{4,12},{8,0},{12,4},{16,24},{20,28},{24,16},{28,20},{1,9},{5... | collective-permute-start | bytes 399368 | tf_op jit(solution)/shard_map/ppermute | solution.py:330
  17.9 7.9 %collective-permute-start.2 = (bf16[520,128]{1,0:T(8,128)(2,1)S(1)}, bf16[520,128]{1,0:T(8,128)(2,1)S(1)}, u32[]{:S(2)}, u32[]{:S(2)}) collective-permute-start(bf16[520,128]{1,0:T(8,128)(2,1)S(1)} %get-tuple-element.20), channel_id=1, source_target_pairs={{0,12},{4,8},{8,4},{12,0},{16,28},{20,24},{24,20},{28,16},{1,13},{... | collective-permute-start | bytes 399368 | tf_op jit(solution)/shard_map/ppermute | solution.py:330
  18.1 8.3 %collective-permute-start.3 = (bf16[520,128]{1,0:T(8,128)(2,1)S(1)}, bf16[520,128]{1,0:T(8,128)(2,1)S(1)}, u32[]{:S(2)}, u32[]{:S(2)}) collective-permute-start(bf16[520,128]{1,0:T(8,128)(2,1)S(1)} %get-tuple-element.21), channel_id=1, source_target_pairs={{0,16},{4,20},{8,24},{12,28},{16,0},{20,4},{24,8},{28,12},{1,17},{... | collective-permute-start | bytes 399368 | tf_op jit(solution)/shard_map/ppermute | solution.py:330
  18.1 11.1 %collective-permute-start.4 = (bf16[520,128]{1,0:T(8,128)(2,1)S(1)}, bf16[520,128]{1,0:T(8,128)(2,1)S(1)}, u32[]{:S(2)}, u32[]{:S(2)}) collective-permute-start(bf16[520,128]{1,0:T(8,128)(2,1)S(1)} %get-tuple-element.22), channel_id=1, source_target_pairs={{0,20},{4,16},{8,28},{12,24},{16,4},{20,0},{24,12},{28,8},{1,21},{... | collective-permute-start | bytes 399368 | tf_op jit(solution)/shard_map/ppermute | solution.py:330
  21.4 18.3 %collective-permute-start.5 = (bf16[520,128]{1,0:T(8,128)(2,1)S(1)}, bf16[520,128]{1,0:T(8,128)(2,1)S(1)}, u32[]{:S(2)}, u32[]{:S(2)}) collective-permute-start(bf16[520,128]{1,0:T(8,128)(2,1)S(1)} %get-tuple-element.23), channel_id=1, source_target_pairs={{0,24},{4,28},{8,16},{12,20},{16,8},{20,12},{24,0},{28,4},{1,25},{... | collective-permute-start | bytes 399368 | tf_op jit(solution)/shard_map/ppermute | solution.py:330
  21.6 22.6 %collective-permute-start.6 = (bf16[520,128]{1,0:T(8,128)(2,1)S(1)}, bf16[520,128]{1,0:T(8,128)(2,1)S(1)}, u32[]{:S(2)}, u32[]{:S(2)}) collective-permute-start(bf16[520,128]{1,0:T(8,128)(2,1)S(1)} %get-tuple-element.24), channel_id=1, source_target_pairs={{0,28},{4,24},{8,20},{12,16},{16,12},{20,8},{24,4},{28,0},{1,29},{... | collective-permute-start | bytes 399368 | tf_op jit(solution)/shard_map/ppermute | solution.py:330
  48.0 3.5 %collective-permute-start.7 = (bf16[64,1024]{1,0:T(8,128)(2,1)S(1)}, bf16[64,1024]{1,0:T(8,128)(2,1)S(1)}, u32[]{:S(2)}, u32[]{:S(2)}) collective-permute-start(bf16[64,1024]{1,0:T(8,128)(2,1)S(1)} %get-tuple-element.26), channel_id=1, source_target_pairs={{0,1},{1,0},{2,3},{3,2},{4,5},{5,4},{6,7},{7,6},{8,9},{9,8},{10,11... | collective-permute-start | bytes 393224 | tf_op jit(solution)/shard_map/ppermute | solution.py:330
  49.8 5.0 %collective-permute-start.8 = (bf16[64,1024]{1,0:T(8,128)(2,1)S(1)}, bf16[64,1024]{1,0:T(8,128)(2,1)S(1)}, u32[]{:S(2)}, u32[]{:S(2)}) collective-permute-start(bf16[64,1024]{1,0:T(8,128)(2,1)S(1)} %get-tuple-element.27), channel_id=1, source_target_pairs={{0,2},{1,3},{2,0},{3,1},{4,6},{5,7},{6,4},{7,5},{8,10},{9,11},{10,... | collective-permute-start | bytes 393224 | tf_op jit(solution)/shard_map/ppermute | solution.py:330
  50.1 7.8 %collective-permute-start.9 = (bf16[64,1024]{1,0:T(8,128)(2,1)S(1)}, bf16[64,1024]{1,0:T(8,128)(2,1)S(1)}, u32[]{:S(2)}, u32[]{:S(2)}) collective-permute-start(bf16[64,1024]{1,0:T(8,128)(2,1)S(1)} %get-tuple-element.28), channel_id=1, source_target_pairs={{0,3},{1,2},{2,1},{3,0},{4,7},{5,6},{6,5},{7,4},{8,11},{9,10},{10,... | collective-permute-start | bytes 393224 | tf_op jit(solution)/shard_map/ppermute | solution.py:330

commit v2 on v1

--- a/solution.py
+++ b/solution.py
@@ -14,31 +14,22 @@
 LANES = 128
 SUBLANES = 8
 
-SIN_POLY = (6.283185280261414, -41.34168066806301, 81.602480742862, -76.58128455932604, 39.76072207590882)
-COS_POLY = (
-    0.999999999779904,
-    -19.739208548314995,
-    64.93934655286789,
-    -85.45356819388616,
-    60.14395231405798,
-    -24.98183599569851,
-)
+SIN_POLY = (4.442882919124345, -7.30824568650904, 3.6063542184326933, -0.8461116503732697, 0.10982451642490525)
+COS_POLY = (1.4142134962552284, -6.978850948563788, 5.73946037690675, -1.8835579059841707, 0.3106880275217573)
 
 
 def horner(square, coefficients):
-    value = jnp.full_like(square, coefficients[-1])
-    for coefficient in coefficients[-2::-1]:
+    value = coefficients[-1] * square + coefficients[-2]
+    for coefficient in coefficients[-3::-1]:
         value = value * square + coefficient
     return value
 
 
 def cos_sin_turns(turns):
-    halves = jnp.round(turns * 2.0)
-    rest = turns - halves * 0.5
-    half = halves * 0.5
-    sign = 1.0 - 4.0 * (half - jnp.floor(half))
+    rest = turns - jnp.round(turns)
     square = rest * rest
-    return (horner(square, COS_POLY) * sign, rest * horner(square, SIN_POLY) * sign)
+    sine = rest * horner(square, SIN_POLY)
+    return (1.0 - sine * sine, sine * horner(square, COS_POLY))
 
 
 def compiler_params(mebibytes):
@@ -46,8 +37,7 @@
 
 
 VMEM = pl.BlockSpec(memory_space=pltpu.VMEM)
-SMEM = pl.BlockSpec(memory_space=pltpu.SMEM)
-ANY = pl.BlockSpec(memory_space=pl.ANY)
+HBM = pl.BlockSpec(memory_space=pltpu.HBM)
 
 
 def dft_tables(length):
@@ -167,40 +157,46 @@
     return facet_image[None]
 
 
-def gather_kernel(peers, capacity, me_ref, centers_ref, facet_ref, plane_ref, cell_ref, vis_ref, uvw_ref, kern_ref, *rest):
-    out_refs, (kern_buf, rows_buf, kern_sem) = rest[:peers], rest[peers:]
+def gather_kernel(peers, capacity, centers_hbm, facet_hbm, plane_hbm, cell_hbm, vis_hbm, uvw_hbm, kern_hbm, *rest):
+    out_refs = rest[:peers]
+    centers_ref, facet_ref, plane_ref, cell_ref, vis_ref, uvw_ref, kern_ref, parts_ref, rows_ref, sems = rest[peers:]
     planes, _, depth, cells = kern_ref.shape
     tiles = facet_ref.shape[1]
-    copies = [pltpu.make_async_copy(kern_ref.at[p], kern_buf.at[p], kern_sem.at[p]) for p in range(planes)]
-    for copy in copies:
+    half = tiles // 2
+    groups_of_lanes = depth // LANES
+    small = [
+        pltpu.make_async_copy(source, target, sems.at[i])
+        for i, (source, target) in enumerate(
+            (
+                (centers_hbm, centers_ref),
+                (facet_hbm, facet_ref),
+                (plane_hbm, plane_ref),
+                (vis_hbm, vis_ref),
+                (uvw_hbm, uvw_ref),
+                (cell_hbm, cell_ref),
+            )
+        )
+    ]
+    large = [
+        pltpu.make_async_copy(kern_hbm.at[p], kern_ref.at[p], sems.at[len(small) + p]) for p in range(planes)
+    ]
+    for copy in small + large:
         copy.start()
+    for copy in small[:3]:
+        copy.wait()
     facet = facet_ref[...]
     l_row = jnp.zeros(facet.shape, jnp.float32)
     m_row = jnp.zeros(facet.shape, jnp.float32)
     for f in range(peers):
         hit = facet == f
-        l_row = jnp.where(hit, centers_ref[f, 0], l_row)
-        m_row = jnp.where(hit, centers_ref[f, 1], m_row)
+        l_row = jnp.where(hit, centers_ref[0:1, f : f + 1], l_row)
+        m_row = jnp.where(hit, centers_ref[1:2, f : f + 1], m_row)
     d_row = jnp.sqrt(1.0 - l_row * l_row - m_row * m_row) - 1.0
     plane_row = plane_ref[...].astype(jnp.float32)
     zero_row = jnp.zeros_like(l_row)
     columns = jnp.concatenate([l_row, m_row, d_row, plane_row] + [zero_row] * 4, axis=0).T
-    l_col, m_col, d_col, plane_col = (columns[:, i : i + 1] for i in range(4))
-
-    u = uvw_ref[0].astype(jnp.float32)
-    v = uvw_ref[1].astype(jnp.float32)
-    w = uvw_ref[2].astype(jnp.float32)
-    cosine, sine = cos_sin_turns(l_col * u + m_col * v + d_col * w)
-    real = vis_ref[:, 0, :].astype(jnp.float32)
-    imag = vis_ref[:, 1, :].astype(jnp.float32)
-    rot_real = (real * cosine + imag * sine).astype(jnp.bfloat16)
-    rot_imag = (imag * cosine - real * sine).astype(jnp.bfloat16)
-    rows_buf[:tiles, :depth] = rot_real
-    rows_buf[:tiles, depth:] = -rot_imag
-    rows_buf[tiles:, :depth] = rot_imag
-    rows_buf[tiles:, depth:] = rot_real
-
-    relative = facet ^ me_ref[0]
+
+    relative = facet ^ lax.axis_index("facet")
     lanes = lax.broadcasted_iota(jnp.int32, (tiles, tiles), 1)
     earlier = (lax.broadcasted_iota(jnp.int32, (tiles, tiles), 0) < lanes).astype(jnp.float32).astype(jnp.bfloat16)
     hits = lax.broadcasted_iota(jnp.int32, (peers, tiles), 0) == relative
@@ -208,18 +204,44 @@
     rank = jnp.sum(jnp.where(hits, before, 0.0), axis=0, keepdims=True)
     slot = relative * capacity + rank.astype(jnp.int32)
     slots = peers * capacity
+
+    for copy in small[3:]:
+        copy.wait()
+    parts_ref[...] = vis_ref[...].astype(jnp.float32)
+    patches = []
+    for h in range(2):
+        tile_rows = slice(h * half, (h + 1) * half)
+        l_col, m_col, d_col, plane_col = (
+            jnp.broadcast_to(columns[tile_rows, i : i + 1], (half, LANES)) for i in range(4)
+        )
+        for j in range(groups_of_lanes):
+            lane = slice(j * LANES, (j + 1) * LANES)
+            u, v, w = (uvw_ref[i, tile_rows, lane].astype(jnp.float32) for i in range(3))
+            cosine, sine = cos_sin_turns(l_col * u + m_col * v + d_col * w)
+            first = 2 * (h * half * groups_of_lanes + j)
+            real = parts_ref[pl.ds(first, half, stride=2 * groups_of_lanes), :]
+            imag = parts_ref[pl.ds(first + 1, half, stride=2 * groups_of_lanes), :]
+            rot_real = (real * cosine + imag * sine).astype(jnp.bfloat16)
+            rot_imag = (imag * cosine - real * sine).astype(jnp.bfloat16)
+            right = slice(depth + j * LANES, depth + (j + 1) * LANES)
+            rows_ref[h, :half, lane] = rot_real
+            rows_ref[h, :half, right] = -rot_imag
+            rows_ref[h, half:, lane] = rot_imag
+            rows_ref[h, half:, right] = rot_real
+        total = None
+        for p in range(planes):
+            mask = (plane_col[:, 0:1] == float(p)).astype(jnp.float32).astype(jnp.bfloat16)
+            mask = jnp.concatenate([mask, mask], axis=0)
+            if h == 0:
+                large[p].wait()
+            product = jnp.dot(
+                rows_ref[h] * mask, kern_ref[p].reshape(2 * depth, cells), preferred_element_type=jnp.float32
+            )
+            total = product if total is None else total + product
+        patches.append(jnp.concatenate([total[:half], total[half:]], axis=1).astype(jnp.bfloat16))
+    patches = jnp.concatenate(patches, axis=0)
     placing = lax.broadcasted_iota(jnp.int32, (slots, tiles), 0) == slot
     placing = placing.astype(jnp.float32).astype(jnp.bfloat16)
-
-    total = jnp.zeros((2 * tiles, cells), jnp.float32)
-    plane_two = jnp.concatenate([plane_col, plane_col], axis=0)
-    for p in range(planes):
-        mask = (plane_two == float(p)).astype(jnp.float32).astype(jnp.bfloat16)
-        copies[p].wait()
-        total = total + jnp.dot(
-            rows_buf[...] * mask, kern_buf[p].reshape(2 * depth, cells), preferred_element_type=jnp.float32
-        )
-    patches = jnp.concatenate([total[:tiles], total[tiles:]], axis=1).astype(jnp.bfloat16)
     placed = jnp.dot(placing, patches, preferred_element_type=jnp.float32).astype(jnp.bfloat16)
     cell = cell_ref[...].astype(jnp.float32)
     block_u = jnp.floor(cell * (1.0 / NBLK))
@@ -234,7 +256,7 @@
         out_refs[s][2 * cells // LANES * capacity :, :] = pair[:, rows]
 
 
-def image_kernel(peers, groups, capacity, me_ref, table_ref, *rest):
+def image_kernel(peers, groups, capacity, table_ref, *rest):
     in_refs, out_refs = rest[:peers], rest[peers : peers + groups]
     phases_buf, patch_buf, table_buf = rest[peers + groups :]
     cells = PSIDE * PSIDE
@@ -254,7 +276,7 @@
             patch_buf[below, left] = -imag
             patch_buf[below, right] = real
     for s in range(groups):
-        start = pl.multiple_of((me_ref[0] ^ s) * share, share)
+        start = pl.multiple_of((lax.axis_index("freq") ^ s) * share, share)
         table_buf[s * share : (s + 1) * share, :] = table_ref[pl.ds(start, share), :]
 
     first = 2 * half_tiles * capacity
@@ -336,30 +358,31 @@
     capacity = 4 * tiles // peers
     planes, _, depth, cells = kernels.shape
     payload = jax.ShapeDtypeStruct((2 * cells // LANES * capacity + SUBLANES, LANES), jnp.bfloat16)
-    facet_index = lax.axis_index("facet").reshape(1).astype(jnp.int32)
-    group_index = lax.axis_index("freq").reshape(1).astype(jnp.int32)
+    lanes = depth // LANES
+    vis_rows = visibilities[0].reshape(tiles, 2, lanes, LANES).transpose(0, 2, 1, 3).reshape(-1, LANES)
+    operands = (
+        centers.T,
+        facet_of.reshape(1, tiles),
+        plane_of,
+        cell_of,
+        vis_rows,
+        uvw[0].transpose(1, 0, 2),
+        kernels,
+    )
     pieces = pl.pallas_call(
         functools.partial(gather_kernel, peers, capacity),
         out_shape=[payload] * peers,
-        in_specs=[SMEM, SMEM, VMEM, VMEM, VMEM, VMEM, VMEM, ANY],
+        in_specs=[HBM] * len(operands),
         out_specs=[VMEM] * peers,
-        scratch_shapes=[
-            pltpu.VMEM(kernels.shape, jnp.bfloat16),
-            pltpu.VMEM((2 * tiles, 2 * depth), jnp.bfloat16),
-            pltpu.SemaphoreType.DMA((planes,)),
+        scratch_shapes=[pltpu.VMEM(operand.shape, operand.dtype) for operand in operands]
+        + [
+            pltpu.VMEM(vis_rows.shape, jnp.float32),
+            pltpu.VMEM((2, tiles, 2 * depth), jnp.bfloat16),
+            pltpu.SemaphoreType.DMA((len(operands) - 1 + planes,)),
         ],
         compiler_params=compiler_params(40),
         name="gather",
-    )(
-        facet_index,
-        centers,
-        facet_of.reshape(1, tiles),
-        plane_of,
-        cell_of,
-        visibilities[0],
-        uvw[0].transpose(1, 0, 2),
-        kernels,
-    )
+    )(*(pltpu.with_memory_space_constraint(operand, pltpu.HBM) for operand in operands))
     received = [pieces[0]] + [swap(pieces[s], "facet", s) for s in range(1, peers)]
     share = cells // groups
     image = jax.ShapeDtypeStruct((share, NBLK * NBLK), jnp.bfloat16)
@@ -367,7 +390,7 @@
     images = pl.pallas_call(
         functools.partial(image_kernel, peers, groups, capacity),
         out_shape=[image] * groups,
-        in_specs=[SMEM] + [VMEM] * (1 + peers),
+        in_specs=[VMEM] * (1 + peers),
         out_specs=[VMEM] * groups,
         scratch_shapes=[
             pltpu.VMEM((2, 8 * NBLK, 2 * slots), jnp.bfloat16),
@@ -376,7 +399,7 @@
         ],
         compiler_params=compiler_params(40),
         name="image",
-    )(group_index, jnp.asarray(patch_table(groups), jnp.bfloat16), *received)
+    )(jnp.asarray(patch_table(groups), jnp.bfloat16), *received)
     summed = [images[0]] + [swap(images[s], "freq", s) for s in range(1, groups)]
     facet_image = pl.pallas_call(
         functools.partial(finish_kernel, groups),

time: 59.2 us -> 51.6 us (0.87)
  local copies, waits for them, and re-layouts: 7.15 us -> 0.01 us
    unnamed x15 -> x2, local copies, waits for them, and re-layouts: 7.15 us -> 0.01 us
where the time goes in v2:
time: 51.6 us; the launch traced here: 51.4 us
  waiting for transfers between devices  27.7 us (54%)
  Pallas kernels  12.7 us (25%)
  starting transfers between devices  11 us (21%)
    ppermute x10, waiting for transfers between devices, swap(): return lax.ppermute(piece, axis, [(i, i ^ distance) for i in range(count)])  27.7 us
    ppermute x10, starting transfers between devices, swap(): return lax.ppermute(piece, axis, [(i, i ^ distance) for i in range(count)])  11 us
    pallas_call x1, Pallas kernels, packed_shards(): pl.pallas_call(functools.partial(gather_kernel, peers, capacity), out_sha...  7.86 us
    pallas_call x1, Pallas kernels, packed_shards(): pl.pallas_call(functools.partial(image_kernel, peers, groups, capacity),...  3.76 us
    pallas_call x1, Pallas kernels, packed_shards(): pl.pallas_call(functools.partial(finish_kernel, groups), out_shape=jax.Sh...  1.07 us
  transfers between devices with their start and end apart: 10, of which 7 were waited for; matrix products, arithmetic and copies ran while one was open for 0% of the time, Pallas kernels for 0%

profile of v2, /device:TPU:19, one launch (start us, length us, event | category | flops | bytes accessed | tf_op | source)
XLA Modules:
  0.0 51.4 jit_solution(8791253715171010721)
XLA Ops:
  0.0 0.0 copy-start
  0.0 7.9 %gather.1 = (bf16[520,128]{1,0:T(8,128)(2,1)S(1)}, bf16[520,128]{1,0:T(8,128)(2,1)S(1)}, bf16[520,128]{1,0:T(8,128)(2,1)S(1)}, bf16[520,128]{1,0:T(8,128)(2,1)S(...) custom-call(f32[2,8]{1,0:T(2,128)} %bitcast.13, ...), custom_call_target="tpu_custom_call" | custom-call | tf_op jit(solution)/shard_map/gather/pallas_call | solution.py:372
  7.9 1.3 %collective-permute-start = (bf16[520,128]{1,0:T(8,128)(2,1)S(1)}, bf16[520,128]{1,0:T(8,128)(2,1)S(1)}, u32[]{:S(2)}, u32[]{:S(2)}) collective-permute-start(bf16[520,128]{1,0:T(8,128)(2,1)S(1)} %get-tuple-element.18), channel_id=1, source_target_pairs={{0,4},{4,0},{8,12},{12,8},{16,20},{20,16},{24,28},{28,24},{1,5},{5... | collective-permute-start | bytes 399368 | tf_op jit(solution)/shard_map/ppermute | solution.py:352
  9.2 1.3 %collective-permute-start.1 = (bf16[520,128]{1,0:T(8,128)(2,1)S(1)}, bf16[520,128]{1,0:T(8,128)(2,1)S(1)}, u32[]{:S(2)}, u32[]{:S(2)}) collective-permute-start(bf16[520,128]{1,0:T(8,128)(2,1)S(1)} %get-tuple-element.19), channel_id=1, source_target_pairs={{0,8},{4,12},{8,0},{12,4},{16,24},{20,28},{24,16},{28,20},{1,9},{5... | collective-permute-start | bytes 399368 | tf_op jit(solution)/shard_map/ppermute | solution.py:352
  10.5 0.1 collective-permute-start.2
  10.6 0.0 collective-permute-start.3
  10.6 3.3 %collective-permute-start.4 = (bf16[520,128]{1,0:T(8,128)(2,1)S(1)}, bf16[520,128]{1,0:T(8,128)(2,1)S(1)}, u32[]{:S(2)}, u32[]{:S(2)}) collective-permute-start(bf16[520,128]{1,0:T(8,128)(2,1)S(1)} %get-tuple-element.22), channel_id=1, source_target_pairs={{0,20},{4,16},{8,28},{12,24},{16,4},{20,0},{24,12},{28,8},{1,21},{... | collective-permute-start | bytes 399368 | tf_op jit(solution)/shard_map/ppermute | solution.py:352
  13.9 0.0 collective-permute-done.rest_1_
  13.9 0.2 collective-permute-start.5
  14.1 0.0 collective-permute-done.1.rest_2_
  14.1 1.2 %collective-permute-start.6 = (bf16[520,128]{1,0:T(8,128)(2,1)S(1)}, bf16[520,128]{1,0:T(8,128)(2,1)S(1)}, u32[]{:S(2)}, u32[]{:S(2)}) collective-permute-start(bf16[520,128]{1,0:T(8,128)(2,1)S(1)} %get-tuple-element.24), channel_id=1, source_target_pairs={{0,28},{4,24},{8,20},{12,16},{16,12},{20,8},{24,4},{28,0},{1,29},{... | collective-permute-start | bytes 399368 | tf_op jit(solution)/shard_map/ppermute | solution.py:352
  15.3 3.0 %collective-permute-done.2.rest_3_ = bf16[520,128]{1,0:T(8,128)(2,1)S(1)} collective-permute-done((bf16[520,128]{1,0:T(8,128)(2,1)S(1)}, bf16[520,128]{1,0:T(8,128)(2,1)S(1)}, u32[]{:S(2)}, u32[]{:S(2)}) %collective-permute-start.2) | collective-permute-done | bytes 133152 | tf_op jit(solution)/shard_map/ppermute | solution.py:352
  18.4 0.6 %collective-permute-done.3.rest_4_ = bf16[520,128]{1,0:T(8,128)(2,1)S(1)} collective-permute-done((bf16[520,128]{1,0:T(8,128)(2,1)S(1)}, bf16[520,128]{1,0:T(8,128)(2,1)S(1)}, u32[]{:S(2)}, u32[]{:S(2)}) %collective-permute-start.3) | collective-permute-done | bytes 133152 | tf_op jit(solution)/shard_map/ppermute | solution.py:352
  18.9 2.8 %collective-permute-done.4.rest_5_ = bf16[520,128]{1,0:T(8,128)(2,1)S(1)} collective-permute-done((bf16[520,128]{1,0:T(8,128)(2,1)S(1)}, bf16[520,128]{1,0:T(8,128)(2,1)S(1)}, u32[]{:S(2)}, u32[]{:S(2)}) %collective-permute-start.4) | collective-permute-done | bytes 133152 | tf_op jit(solution)/shard_map/ppermute | solution.py:352
  21.7 10.5 %collective-permute-done.5.rest_6_ = bf16[520,128]{1,0:T(8,128)(2,1)S(1)} collective-permute-done((bf16[520,128]{1,0:T(8,128)(2,1)S(1)}, bf16[520,128]{1,0:T(8,128)(2,1)S(1)}, u32[]{:S(2)}, u32[]{:S(2)}) %collective-permute-start.5) | collective-permute-done | bytes 133152 | tf_op jit(solution)/shard_map/ppermute | solution.py:352
  32.2 4.5 %collective-permute-done.6.rest_7_ = bf16[520,128]{1,0:T(8,128)(2,1)S(1)} collective-permute-done((bf16[520,128]{1,0:T(8,128)(2,1)S(1)}, bf16[520,128]{1,0:T(8,128)(2,1)S(1)}, u32[]{:S(2)}, u32[]{:S(2)}) %collective-permute-start.6) | collective-permute-done | bytes 133152 | tf_op jit(solution)/shard_map/ppermute | solution.py:352
  36.7 0.0 copy-done
  36.7 3.8 %image.1 = (bf16[64,1024]{1,0:T(8,128)(2,1)S(1)}, bf16[64,1024]{1,0:T(8,128)(2,1)S(1)}, bf16[64,1024]{1,0:T(8,128)(2,1)S(1)}, bf16[64,1024]{1,0:T(8,128)(2,1)S(1)}) custom-call(bf16[256,512]{1,0:T(8,128)(2,1)S(1)} %copy-done, bf16[520,128]{1,0:T(8,128)(2,1)S(1)} %get-tuple-element.17.rest_0_, bf16[520,128]{1,0:T(8,128)(2,1)S(1)} %collective-permute-done.rest_1_, ...), custom_call_target="tpu_custom_call" | custom-call | tf_op jit(solution)/shard_map/image/pallas_call | solution.py:390
  40.5 1.8 %collective-permute-start.7 = (bf16[64,1024]{1,0:T(8,128)(2,1)S(1)}, bf16[64,1024]{1,0:T(8,128)(2,1)S(1)}, u32[]{:S(2)}, u32[]{:S(2)}) collective-permute-start(bf16[64,1024]{1,0:T(8,128)(2,1)S(1)} %get-tuple-element.26), channel_id=1, source_target_pairs={{0,1},{1,0},{2,3},{3,2},{4,5},{5,4},{6,7},{7,6},{8,9},{9,8},{10,11... | collective-permute-start | bytes 393224 | tf_op jit(solution)/shard_map/ppermute | solution.py:352
  42.3 0.2 collective-permute-start.8
  42.6 1.5 %collective-permute-start.9 = (bf16[64,1024]{1,0:T(8,128)(2,1)S(1)}, bf16[64,1024]{1,0:T(8,128)(2,1)S(1)}, u32[]{:S(2)}, u32[]{:S(2)}) collective-permute-start(bf16[64,1024]{1,0:T(8,128)(2,1)S(1)} %get-tuple-element.28), channel_id=1, source_target_pairs={{0,3},{1,2},{2,1},{3,0},{4,7},{5,6},{6,5},{7,4},{8,11},{9,10},{10,... | collective-permute-start | bytes 393224 | tf_op jit(solution)/shard_map/ppermute | solution.py:352
  44.0 0.0 collective-permute-done.7.refs_1_
  44.0 3.3 %collective-permute-done.8.refs_2_ = bf16[64,1024]{1,0:T(8,128)(2,1)S(1)} collective-permute-done((bf16[64,1024]{1,0:T(8,128)(2,1)S(1)}, bf16[64,1024]{1,0:T(8,128)(2,1)S(1)}, u32[]{:S(2)}, u32[]{:S(2)}) %collective-permute-start.8) | collective-permute-done | bytes 131104 | tf_op jit(solution)/shard_map/ppermute | solution.py:352
  47.3 3.1 %collective-permute-done.9.refs_3_ = bf16[64,1024]{1,0:T(8,128)(2,1)S(1)} collective-permute-done((bf16[64,1024]{1,0:T(8,128)(2,1)S(1)}, bf16[64,1024]{1,0:T(8,128)(2,1)S(1)}, u32[]{:S(2)}, u32[]{:S(2)}) %collective-permute-start.9) | collective-permute-done | bytes 131104 | tf_op jit(solution)/shard_map/ppermute | solution.py:352
  50.4 1.1 %finish.1 = f32[512,128]{1,0:T(8,128)} custom-call(bf16[64,1024]{1,0:T(8,128)(2,1)S(1)} %get-tuple-element.25.refs_0_, bf16[64,1024]{1,0:T(8,128)(2,1)S(1)} %collective-permute-done.7.refs_1_, bf16[64,1024]{1,0:T(8,128)(2,1)S(1)} %collective-permute-done.8.refs_2_, bf16[64,1024]{1,0:T(8,128)(2,1)S(1)} %collective-permute-done.9.refs_3_), custom_call_target="tpu_custom_call" | custom-call | tf_op jit(solution)/shard_map/finish/pallas_call | solution.py:404
Async XLA Ops:
  0.0 36.7 %copy-start = (bf16[256,512]{1,0:T(8,128)(2,1)S(1)}, bf16[256,512]{1,0:T(8,128)(2,1)}, u32[]{:S(2)}) copy-start(bf16[256,512]{1,0:T(8,128)(2,1)} %constant.2.clone.table_ref) | copy-start | bytes 786436
  7.9 6.0 %collective-permute-start = (bf16[520,128]{1,0:T(8,128)(2,1)S(1)}, bf16[520,128]{1,0:T(8,128)(2,1)S(1)}, u32[]{:S(2)}, u32[]{:S(2)}) collective-permute-start(bf16[520,128]{1,0:T(8,128)(2,1)S(1)} %get-tuple-element.18), channel_id=1, source_target_pairs={{0,4},{4,0},{8,12},{12,8},{16,20},{20,16},{24,28},{28,24},{1,5},{5... | collective-permute-start | bytes 399368 | tf_op jit(solution)/shard_map/ppermute | solution.py:352
  9.2 4.9 %collective-permute-start.1 = (bf16[520,128]{1,0:T(8,128)(2,1)S(1)}, bf16[520,128]{1,0:T(8,128)(2,1)S(1)}, u32[]{:S(2)}, u32[]{:S(2)}) collective-permute-start(bf16[520,128]{1,0:T(8,128)(2,1)S(1)} %get-tuple-element.19), channel_id=1, source_target_pairs={{0,8},{4,12},{8,0},{12,4},{16,24},{20,28},{24,16},{28,20},{1,9},{5... | collective-permute-start | bytes 399368 | tf_op jit(solution)/shard_map/ppermute | solution.py:352
  10.5 7.9 %collective-permute-start.2 = (bf16[520,128]{1,0:T(8,128)(2,1)S(1)}, bf16[520,128]{1,0:T(8,128)(2,1)S(1)}, u32[]{:S(2)}, u32[]{:S(2)}) collective-permute-start(bf16[520,128]{1,0:T(8,128)(2,1)S(1)} %get-tuple-element.20), channel_id=1, source_target_pairs={{0,12},{4,8},{8,4},{12,0},{16,28},{20,24},{24,20},{28,16},{1,13},{... | collective-permute-start | bytes 399368 | tf_op jit(solution)/shard_map/ppermute | solution.py:352
  10.6 8.3 %collective-permute-start.3 = (bf16[520,128]{1,0:T(8,128)(2,1)S(1)}, bf16[520,128]{1,0:T(8,128)(2,1)S(1)}, u32[]{:S(2)}, u32[]{:S(2)}) collective-permute-start(bf16[520,128]{1,0:T(8,128)(2,1)S(1)} %get-tuple-element.21), channel_id=1, source_target_pairs={{0,16},{4,20},{8,24},{12,28},{16,0},{20,4},{24,8},{28,12},{1,17},{... | collective-permute-start | bytes 399368 | tf_op jit(solution)/shard_map/ppermute | solution.py:352
  10.6 11.1 %collective-permute-start.4 = (bf16[520,128]{1,0:T(8,128)(2,1)S(1)}, bf16[520,128]{1,0:T(8,128)(2,1)S(1)}, u32[]{:S(2)}, u32[]{:S(2)}) collective-permute-start(bf16[520,128]{1,0:T(8,128)(2,1)S(1)} %get-tuple-element.22), channel_id=1, source_target_pairs={{0,20},{4,16},{8,28},{12,24},{16,4},{20,0},{24,12},{28,8},{1,21},{... | collective-permute-start | bytes 399368 | tf_op jit(solution)/shard_map/ppermute | solution.py:352
  13.9 18.3 %collective-permute-start.5 = (bf16[520,128]{1,0:T(8,128)(2,1)S(1)}, bf16[520,128]{1,0:T(8,128)(2,1)S(1)}, u32[]{:S(2)}, u32[]{:S(2)}) collective-permute-start(bf16[520,128]{1,0:T(8,128)(2,1)S(1)} %get-tuple-element.23), channel_id=1, source_target_pairs={{0,24},{4,28},{8,16},{12,20},{16,8},{20,12},{24,0},{28,4},{1,25},{... | collective-permute-start | bytes 399368 | tf_op jit(solution)/shard_map/ppermute | solution.py:352
  14.1 22.7 %collective-permute-start.6 = (bf16[520,128]{1,0:T(8,128)(2,1)S(1)}, bf16[520,128]{1,0:T(8,128)(2,1)S(1)}, u32[]{:S(2)}, u32[]{:S(2)}) collective-permute-start(bf16[520,128]{1,0:T(8,128)(2,1)S(1)} %get-tuple-element.24), channel_id=1, source_target_pairs={{0,28},{4,24},{8,20},{12,16},{16,12},{20,8},{24,4},{28,0},{1,29},{... | collective-permute-start | bytes 399368 | tf_op jit(solution)/shard_map/ppermute | solution.py:352
  40.5 3.5 %collective-permute-start.7 = (bf16[64,1024]{1,0:T(8,128)(2,1)S(1)}, bf16[64,1024]{1,0:T(8,128)(2,1)S(1)}, u32[]{:S(2)}, u32[]{:S(2)}) collective-permute-start(bf16[64,1024]{1,0:T(8,128)(2,1)S(1)} %get-tuple-element.26), channel_id=1, source_target_pairs={{0,1},{1,0},{2,3},{3,2},{4,5},{5,4},{6,7},{7,6},{8,9},{9,8},{10,11... | collective-permute-start | bytes 393224 | tf_op jit(solution)/shard_map/ppermute | solution.py:352
  42.3 5.0 %collective-permute-start.8 = (bf16[64,1024]{1,0:T(8,128)(2,1)S(1)}, bf16[64,1024]{1,0:T(8,128)(2,1)S(1)}, u32[]{:S(2)}, u32[]{:S(2)}) collective-permute-start(bf16[64,1024]{1,0:T(8,128)(2,1)S(1)} %get-tuple-element.27), channel_id=1, source_target_pairs={{0,2},{1,3},{2,0},{3,1},{4,6},{5,7},{6,4},{7,5},{8,10},{9,11},{10,... | collective-permute-start | bytes 393224 | tf_op jit(solution)/shard_map/ppermute | solution.py:352
  42.6 7.8 %collective-permute-start.9 = (bf16[64,1024]{1,0:T(8,128)(2,1)S(1)}, bf16[64,1024]{1,0:T(8,128)(2,1)S(1)}, u32[]{:S(2)}, u32[]{:S(2)}) collective-permute-start(bf16[64,1024]{1,0:T(8,128)(2,1)S(1)} %get-tuple-element.28), channel_id=1, source_target_pairs={{0,3},{1,2},{2,1},{3,0},{4,7},{5,6},{6,5},{7,4},{8,11},{9,10},{10,... | collective-permute-start | bytes 393224 | tf_op jit(solution)/shard_map/ppermute | solution.py:352
